TPU v7x, 32 devices: a whole 2x2x4 slice. The times are simulated.
32 devices in a mesh: row: 4 (over y, core), col: 8 (over z, x).
Axes of the slice: x: 2, y: 2, z: 4, core: 2. Of those that a mesh axis runs over, the one named last changes fastest.
Arguments:
- tokens: bfloat16 [64, 16384], P('row', 'col'), may hold values from -6 to 6
- gate_weight: bfloat16 [16384, 26624], P('col', 'row'), may hold values from -0.046875 to 0.046875
- up_weight: bfloat16 [16384, 26624], P('col', 'row'), may hold values from -0.046875 to 0.046875
Outputs:
- hidden: bfloat16 [64, 26624], P(None, 'row')
All inputs are finite; a program needn't handle non-finite values.
Results may differ from a plain program's by a relative error of at most 0.001.
Values may be sent and summed in bfloat16 or wider, within the bound.
A program may use at most 128 MiB of HBM per device.

v0:
```python
import jax
import jax.numpy as jnp
from jax import lax
from jax.sharding import PartitionSpec as P


def local(tokens, gate_weight, up_weight):
    columns = gate_weight.shape[1]
    block_rows = lax.all_gather(tokens, "row", axis=0, tiled=True)
    gate_term = jnp.dot(block_rows, gate_weight, preferred_element_type=jnp.float32)
    up_term = jnp.dot(block_rows, up_weight, preferred_element_type=jnp.float32)
    partial_value = jnp.concatenate([gate_term, up_term], axis=1)
    shared = lax.psum_scatter(partial_value, "col", scatter_dimension=0, tiled=True)
    gated = (jax.nn.silu(shared[:, :columns]) * shared[:, columns:]).astype(jnp.bfloat16)
    hidden = lax.all_gather(gated, "col", axis=0, tiled=True)
    return hidden


def solution(mesh):
    in_specs = (P("row", "col"), P("col", "row"), P("col", "row"))
    out_specs = P(None, "row")
    return jax.shard_map(local, mesh=mesh, in_specs=in_specs, out_specs=out_specs, check_vma=False)
```

profile of v0, /device:TPU:0, one launch (start us, length us, event | category | flops | bytes accessed | tf_op | source)
XLA Modules:
  0.0 158.8 jit_solution(3400078046058396484)
XLA Ops:
  6.5 0.0 reduce-scatter.2.cloned.1.call-start
  6.5 7.4 %all_gather.6 = bf16[64,2048]{1,0:T(8,128)(2,1)S(1)} all-gather(bf16[16,2048]{1,0:T(8,128)(2,1)} %param.3), channel_id=1, replica_groups=mesh['row'=4,'col'=8] {'row'}, dimensions={0}, use_global_device_ids=true | all-gather | bytes 327680 | tf_op jit(solution)/shard_map/all_gather | solution.py:9
  14.0 11.2 %fusion.2 = f32[64,6656]{1,0:T(8,128)S(1)} fusion(bf16[64,2048]{1,0:T(8,128)(2,1)S(1)} %all_gather.6, bf16[2048,6656]{1,0:T(8,128)(2,1)} %param.5), kind=kOutput, calls=%fused_computation.4 | convolution fusion | flops 1744830464 | bytes 29229056 | tf_op jit(solution)/shard_map/dot_general | solution.py:11
  25.2 11.2 %fusion.1 = f32[64,6656]{1,0:T(8,128)S(1)} fusion(bf16[64,2048]{1,0:T(8,128)(2,1)S(1)} %all_gather.6, bf16[2048,6656]{1,0:T(8,128)(2,1)} %param.4), kind=kOutput, calls=%fused_computation.3 | convolution fusion | flops 1744830464 | bytes 29229056 | tf_op jit(solution)/shard_map/dot_general | solution.py:10
  36.4 2.0 %pad_maximum_fusion = f32[64,13312]{1,0:T(8,128)} fusion(f32[64,6656]{1,0:T(8,128)S(1)} %fusion.2, f32[64,6656]{1,0:T(8,128)S(1)} %fusion.1), kind=kLoop, calls=%fused_computation | loop fusion | flops 851968 | bytes 6815744 | tf_op jit(solution)/shard_map/concatenate | solution.py:12
  38.4 0.0 reduce-scatter.2.cloned.1.call-update
  38.4 79.3 %reduce-scatter.2.cloned.1.call-done = f32[8,13312]{1,0:T(8,128)} async-done(((f32[64,13312]{1,0:T(8,128)}), f32[8,13312]{1,0:T(8,128)}) %reduce-scatter.2.cloned.1.call-update) | async-done | bytes 426000 | tf_op jit(solution)/shard_map/reduce_scatter | solution.py:13
  117.7 1.1 fusion
  118.8 32.2 %all_gather.7 = bf16[64,6656]{1,0:T(8,128)(2,1)S(1)} all-gather(bf16[8,6656]{1,0:T(8,128)(2,1)S(1)} %fusion), channel_id=1, replica_groups=mesh['row'=4,'col'=8] {'col'}, dimensions={0}, use_global_device_ids=true | all-gather | bytes 958464 | tf_op jit(solution)/shard_map/all_gather | solution.py:15
  151.0 0.9 copy.5
Async XLA Ops:
  6.5 111.2 %reduce-scatter.2.cloned.1.call-start = ((), (), s32[]{:S(2)}) async-start(), calls=%async_computation.1 | async-start | bytes 3833856 | tf_op jit(solution)/shard_map/reduce_scatter | solution.py:13
Sparse Core Ops, SparseCore 0:
  38.5 79.1 reduce-scatter.1
where the time goes:
time: 159 us
  waiting for transfers between devices  79.3 us (50%)
  blocking collectives  39.7 us (25%)
  matrix products  22.4 us (14%)
  between operations  13.4 us (8%)
  other arithmetic  3.05 us (2%)
    reduce_scatter x1, waiting for transfers between devices, local(): lax.psum_scatter(partial_value, 'col', scatter_dimension=0, tiled=True)  79.3 us
    all_gather x1, blocking collectives, local(): hidden = lax.all_gather(gated, 'col', axis=0, tiled=True)  32.2 us
    dot_general x1, matrix products, local(): jnp.dot(block_rows, gate_weight, preferred_element_type=jnp.float32)  11.2 us
    dot_general x1, matrix products, local(): up_term = jnp.dot(block_rows, up_weight, preferred_element_type=jnp.float32)  11.2 us
    all_gather x1, blocking collectives, local(): block_rows = lax.all_gather(tokens, 'row', axis=0, tiled=True)  7.45 us
  transfers between devices with their start and end apart: 1, of which 1 were waited for; matrix products, arithmetic and copies ran while one was open for 0% of the time, Pallas kernels for 0%

commit v1 on v0

v1 whole, which is shorter than its diff:
```python
import functools

import jax
import jax.numpy as jnp
from jax import lax
from jax.experimental import pallas as pl
from jax.experimental.pallas import tpu as pltpu
from jax.sharding import PartitionSpec as P

MESH = pl.DeviceIdType.MESH

BUFFERS = 4
LAG = 2
WIDEST = 512
GATHER_REVERSED = True


def digits_of(n):
    bits = n.bit_length() - 1
    out = [(1, 2)]
    weight = 2
    if SPLIT_Z:
        for _ in range(bits - 1):
            out.append((weight, 2))
            weight *= 2
    elif bits > 1:
        out.append((2, n // 2))
    return out


SPLIT_Z = True


LANES = 128
SPAN, FLOOR = 175.0, -87.0


def across(tile, width):
    return jnp.concatenate([tile] * (width // LANES), axis=1)


def encode(x, inverse):
    size = jnp.exp(jnp.abs(x) * across(inverse * SPAN, x.shape[1]) + FLOOR)
    return jnp.where(x < 0, -size, size).astype(jnp.bfloat16)


def decode(y, peak):
    y = y.astype(jnp.float32)
    size = (jnp.log(jnp.abs(y)) - FLOOR) * across(peak * (1.0 / SPAN), y.shape[1])
    return jnp.where(y < 0, -size, size)


def kernel(n_row, n_col, chunks, width, tok_hbm, gate_hbm, up_hbm, out_hbm, *scratch):
    digits = digits_of(n_col)
    stages = len(digits)
    xg, wbuf, acc = scratch[0:3]
    held = scratch[3 : 3 + stages - 1]
    scratch = scratch[2 + stages :]
    sends, recvs, (gath, ) = scratch[:stages], scratch[stages : 2 * stages], scratch[2 * stages : 2 * stages + 1]
    tok_sem, tok_send, tok_recv, w_sem, out_sem = scratch[2 * stages + 1 : 2 * stages + 6]
    rs_send = scratch[2 * stages + 6 : 3 * stages + 6]
    rs_recv = scratch[3 * stages + 6 : 4 * stages + 6]
    ag_send = scratch[4 * stages + 6 : 5 * stages + 6]
    ag_recv = scratch[5 * stages + 6 : 6 * stages + 6]

    row, col = lax.axis_index("row"), lax.axis_index("col")
    mine = [(col // weight) % radix for weight, radix in digits]

    def peer(stage, offset):
        weight, radix = digits[stage]
        return col + ((mine[stage] + offset) % radix - mine[stage]) * weight

    def weights(c, slot):
        cols = pl.ds(pl.multiple_of(c * width, width), width)
        return [
            pltpu.make_async_copy(hbm.at[:, cols], wbuf.at[slot, k], w_sem.at[slot, k])
            for k, hbm in enumerate((gate_hbm, up_hbm))
        ]

    own = pltpu.make_async_copy(tok_hbm, xg.at[row], tok_sem)
    own.start()
    for c in range(min(BUFFERS, chunks)):
        for copy in weights(c, c):
            copy.start()

    barrier = pltpu.get_barrier_semaphore()
    greeted = 0
    for o in range(1, n_row):
        pl.semaphore_signal(barrier, inc=1, device_id=((row + o) % n_row, col), device_id_type=MESH)
        greeted += 1
    for i, (_, radix) in enumerate(digits):
        for o in range(1, radix):
            pl.semaphore_signal(barrier, inc=1, device_id=(row, peer(i, o)), device_id_type=MESH)
            greeted += 1
    pl.semaphore_wait(barrier, greeted)
    own.wait()

    def token_copy(o, place):
        return pltpu.make_async_remote_copy(
            src_ref=xg.at[place], dst_ref=xg.at[place], send_sem=tok_send.at[o - 1], recv_sem=tok_recv.at[o - 1],
            device_id=((row + o) % n_row, col), device_id_type=MESH)

    for o in range(1, n_row):
        token_copy(o, row).start()
    for o in range(1, n_row):
        token_copy(o, (row + n_row - o) % n_row).wait_recv()
    for o in range(1, n_row):
        token_copy(o, row).wait_send()

    def rs_copy(i, o, c):
        return pltpu.make_async_remote_copy(
            src_ref=sends[i].at[c, o - 1], dst_ref=recvs[i].at[c, o - 1],
            send_sem=rs_send[i].at[o - 1, c], recv_sem=rs_recv[i].at[o - 1, c],
            device_id=(row, peer(i, o)), device_id_type=MESH)

    def send_parts(i, source, c):
        sub = source.shape[1] // digits[i][1]
        for o in range(1, digits[i][1]):
            to = (mine[i] + o) % digits[i][1]
            for k in range(2):
                parts = [source[c, to * sub + g, k] for g in range(sub)]
                peak = functools.reduce(jnp.maximum, [
                    jnp.abs(part[:, at : at + LANES]) for part in parts for at in range(0, width, LANES)])
                peak = jnp.maximum(peak * 1.01, 1e-37).astype(jnp.bfloat16)
                sends[i][c, o - 1, k, :, sub * width :] = peak
                inverse = 1.0 / peak.astype(jnp.float32)
                for g, part in enumerate(parts):
                    sends[i][c, o - 1, k, :, g * width : (g + 1) * width] = encode(part, inverse)
            rs_copy(i, o, c).start()

    def summed(i, source, c, sink):
        sub = source.shape[1] // digits[i][1]
        for o in range(1, digits[i][1]):
            rs_copy(i, o, c).wait_recv()
        for k in range(2):
            peaks = [recvs[i][c, o, k, :, sub * width :].astype(jnp.float32) for o in range(digits[i][1] - 1)]
            for g in range(sub):
                total = source[c, mine[i] * sub + g, k]
                for o, peak in enumerate(peaks):
                    total = total + decode(recvs[i][c, o, k, :, g * width : (g + 1) * width], peak)
                sink(g, k, total)

    order = list(range(stages))[::-1] if GATHER_REVERSED else list(range(stages))

    def gathered_place(a, c, shift):
        index = [c]
        for i in range(stages):
            if i in order[:a]:
                index.append(slice(None))
            elif i == order[a]:
                index.append((mine[i] + digits[i][1] + shift) % digits[i][1])
            else:
                index.append(mine[i])
        return gath.at[tuple(index)]

    def ag_copy(a, o, c, shift):
        ref = gathered_place(a, c, shift)
        return pltpu.make_async_remote_copy(
            src_ref=ref, dst_ref=ref, send_sem=ag_send[a].at[o - 1, c], recv_sem=ag_recv[a].at[o - 1, c],
            device_id=(row, peer(order[a], o)), device_id_type=MESH)

    def ag_start(a, c):
        for o in range(1, digits[order[a]][1]):
            ag_copy(a, o, c, 0).start()

    def ag_wait(a, c):
        for o in range(1, digits[order[a]][1]):
            ag_copy(a, o, c, -o).wait_recv()

    def out_copy(c):
        cols = pl.ds(pl.multiple_of(c * width, width), width)
        return pltpu.make_async_copy(gath.at[c], out_hbm.at[(slice(None),) * (stages + 1) + (cols,)], out_sem.at[c])

    def multiply(c):
        slot = c % BUFFERS
        for k, copy in enumerate(weights(c, slot)):
            copy.wait()
            x = xg[...].reshape(-1, xg.shape[-1])
            part = jnp.dot(x, wbuf[slot, k], preferred_element_type=jnp.float32)
            acc[c, :, k] = part.reshape(n_col, -1, width)
        send_parts(0, acc, c)

        @pl.when(c + BUFFERS < chunks)
        def _():
            for copy in weights(c + BUFFERS, slot):
                copy.start()

    def reduce_step(i, c):
        source = acc if i == 0 else held[i - 1]
        if i < stages - 1:
            def keep(g, k, total):
                held[i][c, g, k] = total

            summed(i, source, c, keep)
            send_parts(i + 1, held[i], c)
        else:
            sums = []
            summed(i, source, c, lambda g, k, total: sums.append(total))
            gate, up = sums
            gath[(c, *mine)] = (gate / (1.0 + jnp.exp(-gate)) * up).astype(jnp.bfloat16)
            ag_start(0, c)

    def gather_step(a, c):
        ag_wait(a, c)
        if a < stages - 1:
            ag_start(a + 1, c)
        else:
            out_copy(c).start()

    steps = [multiply]
    steps += [functools.partial(reduce_step, i) for i in range(stages)]
    steps += [functools.partial(gather_step, a) for a in range(stages)]

    def turn(t, carry):
        for s, step in enumerate(steps):
            c = t - s * LAG

            @pl.when(jnp.logical_and(c >= 0, c < chunks))
            def _(c=c, step=step):
                step(c)

        return carry

    lax.fori_loop(0, chunks + (len(steps) - 1) * LAG, turn, 0)

    def drain(c, carry):
        for i in range(stages):
            for o in range(1, digits[i][1]):
                rs_copy(i, o, c).wait_send()
        for a in range(stages):
            for o in range(1, digits[order[a]][1]):
                ag_copy(a, o, c, 0).wait_send()
        out_copy(c).wait()
        return carry

    lax.fori_loop(0, chunks, drain, 0)


def solution(mesh):
    n_row, n_col = mesh.shape["row"], mesh.shape["col"]

    def local(tokens, gate_weight, up_weight):
        own_tokens, depth = tokens.shape
        columns = gate_weight.shape[1]
        each = own_tokens * n_row // n_col
        width = max(w for w in range(128, WIDEST + 1, 128) if columns % w == 0)
        chunks = columns // width
        digits = digits_of(n_col)
        radices = tuple(radix for _, radix in digits)
        subs, count = [], n_col
        for radix in radices:
            count //= radix
            subs.append(count)
        parts = [(chunks, radix - 1, 2, each, sub * width + LANES) for radix, sub in zip(radices, subs)]
        scratch = [
            pltpu.VMEM((n_row, own_tokens, depth), jnp.bfloat16),
            pltpu.VMEM((BUFFERS, 2, depth, width), jnp.bfloat16),
            pltpu.VMEM((chunks, n_col, 2, each, width), jnp.float32),
        ]
        scratch += [pltpu.VMEM((chunks, sub, 2, each, width), jnp.float32) for sub in subs[:-1]]
        scratch += [pltpu.VMEM(shape, jnp.bfloat16) for shape in parts]
        scratch += [pltpu.VMEM(shape, jnp.bfloat16) for shape in parts]
        scratch += [pltpu.VMEM((chunks, *radices, each, width), jnp.bfloat16)]
        dma = pltpu.SemaphoreType.DMA
        scratch += [dma, dma((n_row - 1,)), dma((n_row - 1,)), dma((BUFFERS, 2)), dma((chunks,))]
        for _ in range(2):
            scratch += [dma((radix - 1, chunks)) for radix in radices]
        ordered = radices[::-1] if GATHER_REVERSED else radices
        for _ in range(2):
            scratch += [dma((radix - 1, chunks)) for radix in ordered]
        out = pl.pallas_call(
            functools.partial(kernel, n_row, n_col, chunks, width),
            out_shape=jax.ShapeDtypeStruct((*radices, each, columns), jnp.bfloat16),
            in_specs=[pl.BlockSpec(memory_space=pl.ANY)] * 3,
            out_specs=pl.BlockSpec(memory_space=pl.ANY),
            scratch_shapes=scratch,
            compiler_params=pltpu.CompilerParams(
                collective_id=0, has_side_effects=True, vmem_limit_bytes=60 * 2**20),
        )(tokens, gate_weight, up_weight)
        return out.reshape(n_col * each, columns)

    in_specs = (P("row", "col"), P("col", "row"), P("col", "row"))
    return jax.shard_map(local, mesh=mesh, in_specs=in_specs, out_specs=P(None, "row"), check_vma=False)
```

time: 159 us -> 59.3 us (0.37)
  waiting for transfers between devices: 79.3 us -> 0 us
  Pallas kernels: 0 us -> 57 us
  blocking collectives: 39.7 us -> 0 us
  matrix products: 22.4 us -> 0 us
  between operations: 13.4 us -> 0.01 us
  other arithmetic: 3.05 us -> 0 us
    reduce_scatter x1 -> x0, waiting for transfers between devices: 79.3 us -> none  [local(): lax.psum_scatter(partial_value, 'col', scatter_dimension=0, tiled=True)]
    pallas_call x0 -> x1, Pallas kernels: none -> 57 us  [local(): pl.pallas_call(functools.partial(kernel, n_row, n_col, chunks, width), ou...]
    all_gather x2 -> x0, blocking collectives: 39.7 us -> none  [the longest x1 32.2 us: local(): hidden = lax.all_gather(gated, 'col', axis=0, tiled=True)]
    dot_general x2 -> x0, matrix products: 22.4 us -> none  [the longest x1 11.2 us: local(): jnp.dot(block_rows, gate_weight, preferred_element_type=jnp.float32)]
    concatenate x1 -> x0, other arithmetic: 1.95 us -> none  [local(): partial_value = jnp.concatenate([gate_term, up_term], axis=1)]
  transfers between devices with their start and end apart: 1 -> 0, of which waited for: 1 -> 0; matrix products, arithmetic and copies ran while one was open for 0% -> 0% of each run, Pallas kernels for 0% -> 0%
where the time goes in v1:
time: 59.3 us; the launch traced here: 59.1 us
  Pallas kernels  57 us (96%)
  local copies, waits for them, and re-layouts  2.11 us (4%)
    pallas_call x1, Pallas kernels, local(): pl.pallas_call(functools.partial(kernel, n_row, n_col, chunks, width), ou...  57 us
    unnamed x1, local copies, waits for them, and re-layouts  2.11 us

profile of v1, /device:TPU:0, one launch (start us, length us, event | category | flops | bytes accessed | tf_op | source)
XLA Modules:
  0.0 59.1 jit_solution(14928211240158579022)
XLA Ops:
  0.0 57.0 %shard_map.37 = bf16[2,2,2,8,6656]{4,3,2,1,0:T(8,128)(2,1)} custom-call(bf16[16,2048]{1,0:T(8,128)(2,1)} %tok_hbm.1, bf16[2048,6656]{1,0:T(8,128)(2,1)} %gate_hbm.1, bf16[2048,6656]{1,0:T(8,128)(2,1)} %up_hbm.1), custom_call_target="tpu_custom_call" | custom-call | tf_op jit(solution)/shard_map/pallas_call | solution.py:271
  57.0 2.1 %copy.5 = bf16[64,6656]{1,0:T(8,128)(2,1)} copy(bf16[64,6656]{1,0:T(8,128)(2,1)} %bitcast.1) | data formatting | bytes 1703936

commit v2 on v1

--- a/solution.py
+++ b/solution.py
@@ -10,7 +10,7 @@
 MESH = pl.DeviceIdType.MESH
 
 BUFFERS = 4
-LAG = 2
+LAG = 3
 WIDEST = 512
 GATHER_REVERSED = True
 

time: 59.3 us -> 57.3 us (0.966)
  Pallas kernels: 57 us -> 55 us
    pallas_call x1, Pallas kernels: 57 us -> 55 us  [local(): pl.pallas_call(functools.partial(kernel, n_row, n_col, chunks, width), ou...]
where the time goes in v2:
time: 57.3 us; the launch traced here: 57.1 us
  Pallas kernels  55 us (96%)
  local copies, waits for them, and re-layouts  2.11 us (4%)
    pallas_call x1, Pallas kernels, local(): pl.pallas_call(functools.partial(kernel, n_row, n_col, chunks, width), ou...  55 us
    unnamed x1, local copies, waits for them, and re-layouts  2.11 us

profile of v2, /device:TPU:0, one launch (start us, length us, event | category | flops | bytes accessed | tf_op | source)
XLA Modules:
  0.0 57.1 jit_solution(1674471306163616208)
XLA Ops:
  0.0 55.0 %shard_map.37 = bf16[2,2,2,8,6656]{4,3,2,1,0:T(8,128)(2,1)} custom-call(bf16[16,2048]{1,0:T(8,128)(2,1)} %tok_hbm.1, bf16[2048,6656]{1,0:T(8,128)(2,1)} %gate_hbm.1, bf16[2048,6656]{1,0:T(8,128)(2,1)} %up_hbm.1), custom_call_target="tpu_custom_call" | custom-call | tf_op jit(solution)/shard_map/pallas_call | solution.py:271
  55.0 2.1 %copy.5 = bf16[64,6656]{1,0:T(8,128)(2,1)} copy(bf16[64,6656]{1,0:T(8,128)(2,1)} %bitcast.1) | data formatting | bytes 1703936
